TPU v7x, 32 devices: a whole 2x2x4 slice. The times are simulated.
32 devices in a mesh: ctx: 8 (over y, x, core), head: 4 (over z).
Axes of the slice: x: 2, y: 2, z: 4, core: 2. Of those that a mesh axis runs over, the one named last changes fastest.
Arguments:
- query_nope: bfloat16 [1024, 8192], P('ctx', 'head'), may hold values from -6 to 6
- query_rope: bfloat16 [1024, 4096], P('ctx', 'head'), may hold values from -450 to 450
- grad_out: bfloat16 [1024, 8192], P('ctx', 'head'), may hold values from -24 to 24
- latent: bfloat16 [1024, 576], P(('ctx', 'head')), may hold values from -8 to 8
- key_up: bfloat16 [512, 8192], P(None, 'head'), may hold values from -0.25 to 0.25
- value_up: bfloat16 [512, 8192], P(None, 'head'), may hold values from -0.25 to 0.25
- block_keep: int32 [8, 3], P('ctx'), may hold values 0 or 1
Outputs:
- d_query_nope: float32 [1024, 8192], P('ctx', 'head')
- d_query_rope: float32 [1024, 4096], P('ctx', 'head')
- d_latent: float32 [1024, 576], P(('ctx', 'head'))
All inputs are finite; a program needn't handle non-finite values. No bound on the sum of `block_keep` on one device may be relied on, other than what follows from the above.
Results may differ from a plain program's by a relative error of at most 0.015.
Values may be sent and summed in bfloat16 or wider, within the bound.
A program may use at most 64 MiB of HBM per device.

v0:
```python
import functools
import math

import jax
import jax.numpy as jnp
from jax import lax
from jax.experimental import pallas as pl
from jax.experimental.pallas import tpu as pltpu
from jax.sharding import PartitionSpec as P

NOPE = 128
ROPE = 64
VDIM = 128
RANK = 512
STEPS = 3
BF = jnp.bfloat16
F32 = jnp.float32
MESH = pl.DeviceIdType.MESH
FOR_BACK, FOR_OWN, FROM_NEXT = 0, 1, 2


def dot_nt(a, b):
    return lax.dot_general(a, b, (((1,), (1,)), ((), ())), preferred_element_type=F32)


def dot_tn(a, b):
    return lax.dot_general(a, b, (((0,), (0,)), ((), ())), preferred_element_type=F32)


def kernel(
    n_ctx, n_head,
    keep_ref, lat_ref, qn_hbm, qr_hbm, go_hbm, ku_hbm, vu_hbm,
    dqn_hbm, dqr_hbm, dlat_ref,
    win, qn, qr, go, ku, vu, krlo, krhi, bias, keys, vals, dkeys, dvals, slopes_grad,
    rope_even, rope_odd, dqn, dqr, own, back, parts, got, zparts, zgot,
    load_sem, store_sem, zs_sem, as_sem, bs_sem, cs_sem, win_sem,
    ps_sem, got_sem, ws_sem, zgot_sem,
):
    c = lax.axis_index("ctx")
    h = lax.axis_index("head")
    even = lax.rem(c, 2) == 0
    partner = jnp.where(even, c + 1, c - 1)
    far = jnp.where(even, c - 3, c + 3)
    has_far = (far >= 0) & (far < n_ctx)
    rows = lat_ref.shape[0]
    group = rows * n_head
    span = group * (STEPS + 1)
    heads = qn.shape[1] // NOPE
    scale = 1.0 / math.sqrt(NOPE + ROPE)

    loads = [
        pltpu.make_async_copy(src, dst, load_sem.at[i])
        for i, (src, dst) in enumerate(
            [(ku_hbm, ku), (vu_hbm, vu), (qn_hbm, qn), (qr_hbm, qr), (go_hbm, go)]
        )
    ]
    for load in loads:
        load.start()

    barrier = pltpu.get_barrier_semaphore()
    for t in range(1, n_head):
        pl.semaphore_signal(
            barrier, inc=1, device_id=(c, lax.rem(h + t, n_head)), device_id_type=MESH
        )
    pl.semaphore_signal(barrier, inc=1, device_id=(partner, h), device_id_type=MESH)
    for ok, who in ((c >= 2, c - 2), (c + 2 < n_ctx, c + 2), (has_far, far)):

        @pl.when(ok)
        def _():
            pl.semaphore_signal(barrier, inc=1, device_id=(who, h), device_id_type=MESH)

    peers = n_head
    for ok in (c >= 2, c + 2 < n_ctx, has_far):
        peers = peers + jnp.where(ok, 1, 0)
    pl.semaphore_wait(barrier, peers)

    def piece(t):
        return lax.rem(h - t + n_head, n_head)

    def over_head(t):
        return pltpu.make_async_remote_copy(
            src_ref=lat_ref, dst_ref=win.at[3, h], send_sem=zs_sem.at[t],
            recv_sem=win_sem.at[3, t], device_id=(c, lax.rem(h + t, n_head)),
            device_id_type=MESH,
        )

    def own_source(t):
        return lat_ref if t == 0 else win.at[3, piece(t)]

    def send_two_ahead(t):
        return pltpu.make_async_remote_copy(
            src_ref=own_source(t), dst_ref=win.at[1, piece(t)], send_sem=as_sem.at[t],
            recv_sem=win_sem.at[1, t], device_id=(c + 2, h), device_id_type=MESH,
        )

    b_slot = jnp.where(even, 2, 0)
    b_who = jnp.where(even, c + 1, c + 3)
    b_ok = b_who < n_ctx

    def send_odd_ahead(t):
        return pltpu.make_async_remote_copy(
            src_ref=own_source(t), dst_ref=win.at[b_slot, piece(t)], send_sem=bs_sem.at[t],
            recv_sem=win_sem.at[b_slot, t], device_id=(b_who, h), device_id_type=MESH,
        )

    c_slot = jnp.where(even, 0, 2)

    def forward(t):
        return pltpu.make_async_remote_copy(
            src_ref=win.at[1, piece(t)], dst_ref=win.at[c_slot, piece(t)], send_sem=cs_sem.at[t],
            recv_sem=win_sem.at[c_slot, t], device_id=(partner, h), device_id_type=MESH,
        )

    def wait_piece(slot, t):
        pltpu.make_async_remote_copy(
            src_ref=lat_ref, dst_ref=win.at[slot, piece(t)], send_sem=zs_sem.at[0],
            recv_sem=win_sem.at[slot, t], device_id=(partner, h), device_id_type=MESH,
        ).wait_recv()

    @pl.when(c + 2 < n_ctx)
    def _():
        send_two_ahead(0).start()

    for t in range(1, n_head):
        over_head(t).start()

    @pl.when(b_ok)
    def _():
        send_odd_ahead(0).start()

    own_copy = pltpu.make_async_copy(lat_ref, win.at[3, h], zs_sem.at[0])
    own_copy.start()

    key_at = lax.broadcasted_iota(jnp.int32, (group, group), 0)
    query_at = lax.broadcasted_iota(jnp.int32, (group, group), 1)
    bias[STEPS * group :, :] = jnp.where(key_at <= query_at, 0.0, -jnp.inf).astype(F32)
    for k in range(1, STEPS + 1):
        flag = jnp.where((keep_ref[0, k - 1] == 1) & (c >= k), 0.0, -jnp.inf).astype(F32)
        bias[(STEPS - k) * group : (STEPS - k + 1) * group, :] = jnp.full((group, group), flag, F32)

        @pl.when(c < k)
        def _():
            win[STEPS - k] = jnp.zeros(win.shape[1:], BF)

    rope_even[...] = jnp.zeros(rope_even.shape, F32)
    rope_odd[...] = jnp.zeros(rope_odd.shape, F32)

    for t in range(1, n_head):
        wait_piece(3, t)

        @pl.when(c + 2 < n_ctx)
        def _():
            send_two_ahead(t).start()

        @pl.when(b_ok)
        def _():
            send_odd_ahead(t).start()

    def at_pair(j, width):
        return pl.ds(pl.multiple_of(j * width, width), width)

    def expand(slots):
        size = len(slots) * group
        blocks = jnp.concatenate([win[i : i + 1] for i in slots], axis=0)
        content = blocks[:, :, :, :RANK].reshape(size, RANK)
        rope_keys = blocks[:, :, :, RANK:].reshape(size, ROPE)
        pad = jnp.zeros((size, ROPE), BF)
        low = jnp.concatenate([rope_keys, pad], axis=1)
        high = jnp.concatenate([pad, rope_keys], axis=1)

        def store(ref, lanes, value):
            for i, slot in enumerate(slots):
                ref[slot * group : (slot + 1) * group, lanes] = value[i * group : (i + 1) * group]

        store(krlo, slice(None), low)
        store(krhi, slice(None), high)

        def expand_step(j, carry):
            lanes = at_pair(j, 2 * NOPE)
            store(keys, lanes, jnp.dot(content, ku[:, lanes], preferred_element_type=F32).astype(BF))
            store(vals, lanes, jnp.dot(content, vu[:, lanes], preferred_element_type=F32).astype(BF))
            return carry

        lax.fori_loop(0, heads // 2, expand_step, 0, unroll=min(4, heads // 2))

    own_copy.wait()
    for load in loads:
        load.wait()
    expand((3,))

    @pl.when(c >= 2)
    def _():
        for t in range(n_head):
            wait_piece(1, t)
            forward(t).start()

    expand((1,))
    for k in (1, 3):

        @pl.when(c >= k)
        def _():
            for t in range(n_head):
                wait_piece(STEPS - k, t)

    expand((0, 2))

    def pair_step(j, carry):
        wide = at_pair(j, 2 * NOPE)
        key_pair = keys[:, wide]
        value_pair = vals[:, wide]
        qn_pair = qn[:, wide]
        go_pair = go[:, wide]
        qr_pair = qr[:, at_pair(j, 2 * ROPE)]
        dk, dv = [], []
        for e, (kr, rope_sum) in enumerate(((krlo, rope_even), (krhi, rope_odd))):
            lanes = slice(e * NOPE, (e + 1) * NOPE)
            key = jnp.concatenate([key_pair[:, lanes], kr[...]], axis=1)
            query = jnp.concatenate([qn_pair[:, lanes], qr_pair], axis=1)
            cotangent = go_pair[:, lanes]
            scores = dot_nt(key, query) * scale + bias[...]
            top = jnp.max(scores, axis=0, keepdims=True)
            exponent = jnp.exp(scores - top)
            probs = exponent * (1.0 / jnp.sum(exponent, axis=0, keepdims=True))
            weights = probs.astype(BF)
            slopes = dot_nt(value_pair[:, lanes], cotangent)
            delta = jnp.sum(weights.astype(F32) * slopes, axis=0, keepdims=True)
            score_grad = (probs * ((slopes - delta) * scale)).astype(BF)
            slopes_grad[2 * j + e] = score_grad
            both = jnp.dot(score_grad, query, preferred_element_type=F32)
            dk.append(both[:, :NOPE].astype(BF))
            rope_sum[...] += both[:, NOPE:]
            dv.append(jnp.dot(weights, cotangent, preferred_element_type=F32).astype(BF))
        dkeys[:, wide] = jnp.concatenate(dk, axis=1)
        dvals[:, wide] = jnp.concatenate(dv, axis=1)
        return carry

    lax.fori_loop(0, heads // 2, pair_step, 0, unroll=min(8, heads // 2))

    def terms_of(k):
        at = slice((STEPS - k) * group, (STEPS - k + 1) * group)
        content = dot_nt(dkeys[at, :], ku[...]) + dot_nt(dvals[at, :], vu[...])
        rope = rope_even[at, :ROPE] + rope_odd[at, ROPE:]
        return content.reshape(n_head, rows, RANK), rope.reshape(n_head, rows, ROPE)

    def put(ref, k):
        content, rope = terms_of(k)
        ref[:, :, :RANK] = content.astype(ref.dtype)
        ref[:, :, RANK:] = rope.astype(ref.dtype)

    order = [*range(1, n_head), 0]

    def chunk(t):
        return lax.rem(h + t, n_head)

    def send_part(i, slot, who, t):
        return pltpu.make_async_remote_copy(
            src_ref=parts.at[i, chunk(t)], dst_ref=got.at[slot, chunk(t)], send_sem=ps_sem.at[i, t],
            recv_sem=got_sem.at[slot, t], device_id=(who, h), device_id_type=MESH,
        )

    def part3(t):
        return send_part(0, jnp.where(even, FOR_OWN, FOR_BACK), jnp.where(even, c - 3, c - 1), t)

    def part1(t):
        return send_part(1, jnp.where(even, FOR_BACK, FOR_OWN), partner, t)

    def part2(t):
        return send_part(2, FROM_NEXT, c - 2, t)

    def wait_part(slot, t):
        send_part(0, slot, partner, t).wait_recv()

    put(parts.at[0], 3)

    @pl.when(c >= 3)
    def _():
        for t in order:
            part3(t).start()

    put(parts.at[1], 1)

    @pl.when(c >= 1)
    def _():
        for t in order:
            part1(t).start()

    put(back, 2)

    @pl.when(c >= 2)
    def _():
        for t in order:
            wait_part(FOR_BACK, t)
            parts[2, chunk(t)] = (back[chunk(t)] + got[FOR_BACK, chunk(t)].astype(F32)).astype(BF)
            part2(t).start()

    put(own, 0)

    def dq_step(j, carry):
        wide = at_pair(j, 2 * NOPE)
        key_pair = keys[:, wide]
        nope, rope = [], None
        for e, kr in enumerate((krlo, krhi)):
            key = jnp.concatenate([key_pair[:, e * NOPE : (e + 1) * NOPE], kr[...]], axis=1)
            both = dot_tn(slopes_grad[2 * j + e], key)
            nope.append(both[:, :NOPE])
            rope = both[:, NOPE:] if rope is None else rope + both[:, NOPE:]
        dqn[:, wide] = jnp.concatenate(nope, axis=1)
        dqr[:, at_pair(j, 2 * ROPE)] = rope
        return carry

    lax.fori_loop(0, heads // 2, dq_step, 0)
    stores = [
        pltpu.make_async_copy(dqn, dqn_hbm, store_sem.at[0]),
        pltpu.make_async_copy(dqr, dqr_hbm, store_sem.at[1]),
    ]
    for store in stores:
        store.start()

    own_ok = even | (c + 3 < n_ctx)

    def scatter(t):
        return pltpu.make_async_remote_copy(
            src_ref=zparts.at[chunk(t)], dst_ref=zgot.at[t], send_sem=ws_sem.at[t],
            recv_sem=zgot_sem.at[t], device_id=(c, chunk(t)), device_id_type=MESH,
        )

    for t in order:

        @pl.when(own_ok)
        def _():
            wait_part(FOR_OWN, t)
            own[chunk(t)] += got[FOR_OWN, chunk(t)].astype(F32)

        @pl.when(c + 2 < n_ctx)
        def _():
            wait_part(FROM_NEXT, t)
            own[chunk(t)] += got[FROM_NEXT, chunk(t)].astype(F32)

        if t > 0:
            zparts[chunk(t)] = own[chunk(t)].astype(BF)
            scatter(t).start()

    total = own[h]
    for t in range(1, n_head):
        scatter(t).wait_recv()
        total = total + zgot[t].astype(F32)
    dlat_ref[...] = total

    for t in range(1, n_head):
        scatter(t).wait_send()
        over_head(t).wait_send()

    @pl.when(c + 2 < n_ctx)
    def _():
        for t in range(n_head):
            send_two_ahead(t).wait_send()

    @pl.when(b_ok)
    def _():
        for t in range(n_head):
            send_odd_ahead(t).wait_send()

    @pl.when(c >= 2)
    def _():
        for t in range(n_head):
            forward(t).wait_send()
            part2(t).wait_send()

    @pl.when(c >= 1)
    def _():
        for t in range(n_head):
            part1(t).wait_send()

    @pl.when(c >= 3)
    def _():
        for t in range(n_head):
            part3(t).wait_send()

    for store in stores:
        store.wait()


def on_device(n_ctx, n_head, query_nope, query_rope, grad_out, latent, key_up, value_up, block_keep):
    rows, width = latent.shape
    group = query_nope.shape[0]
    span = group * (STEPS + 1)
    wide = query_nope.shape[1]
    rope_wide = query_rope.shape[1]
    heads = wide // NOPE
    assert block_keep.shape[1] == STEPS and n_ctx % 2 == 0
    vmem, hbm = pl.BlockSpec(memory_space=pltpu.VMEM), pl.BlockSpec(memory_space=pl.ANY)
    dma = pltpu.SemaphoreType.DMA
    block = (n_head, rows, width)
    return pl.pallas_call(
        functools.partial(kernel, n_ctx, n_head),
        out_shape=(
            jax.ShapeDtypeStruct((group, wide), F32),
            jax.ShapeDtypeStruct((group, rope_wide), F32),
            jax.ShapeDtypeStruct((rows, width), F32),
        ),
        in_specs=[pl.BlockSpec(memory_space=pltpu.SMEM), vmem, hbm, hbm, hbm, hbm, hbm],
        out_specs=(hbm, hbm, vmem),
        scratch_shapes=[
            pltpu.VMEM((STEPS + 1,) + block, BF),
            pltpu.VMEM((group, wide), BF),
            pltpu.VMEM((group, rope_wide), BF),
            pltpu.VMEM((group, wide), BF),
            pltpu.VMEM((RANK, wide), BF),
            pltpu.VMEM((RANK, wide), BF),
            pltpu.VMEM((span, 2 * ROPE), BF),
            pltpu.VMEM((span, 2 * ROPE), BF),
            pltpu.VMEM((span, group), F32),
            pltpu.VMEM((span, wide), BF),
            pltpu.VMEM((span, wide), BF),
            pltpu.VMEM((span, wide), BF),
            pltpu.VMEM((span, wide), BF),
            pltpu.VMEM((heads, span, group), BF),
            pltpu.VMEM((span, 2 * ROPE), F32),
            pltpu.VMEM((span, 2 * ROPE), F32),
            pltpu.VMEM((group, wide), F32),
            pltpu.VMEM((group, rope_wide), F32),
            pltpu.VMEM(block, F32),
            pltpu.VMEM(block, F32),
            pltpu.VMEM((3,) + block, BF),
            pltpu.VMEM((3,) + block, BF),
            pltpu.VMEM(block, BF),
            pltpu.VMEM(block, BF),
            dma((5,)),
            dma((2,)),
            dma((n_head,)),
            dma((n_head,)),
            dma((n_head,)),
            dma((n_head,)),
            dma((STEPS + 1, n_head)),
            dma((3, n_head)),
            dma((3, n_head)),
            dma((n_head,)),
            dma((n_head,)),
        ],
        compiler_params=pltpu.CompilerParams(collective_id=0, has_side_effects=True),
        name="latent_attention_grads",
    )(block_keep, latent, query_nope, query_rope, grad_out, key_up, value_up)


def solution(mesh):
    placed = (
        P("ctx", "head"),
        P("ctx", "head"),
        P("ctx", "head"),
        P(("ctx", "head"), None),
        P(None, "head"),
        P(None, "head"),
        P("ctx", None),
    )
    return jax.shard_map(
        functools.partial(on_device, mesh.shape["ctx"], mesh.shape["head"]),
        mesh=mesh,
        in_specs=placed,
        out_specs=(P("ctx", "head"), P("ctx", "head"), P(("ctx", "head"), None)),
        check_vma=False,
    )
```

profile of v0, /device:TPU:0, one launch (start us, length us, event | category | flops | bytes accessed | tf_op | source)
XLA Modules:
  0.0 42.3 jit_solution(5026230086140986563)
XLA Ops:
  0.6 37.8 %latent_attention_grads.1 = (f32[128,2048]{1,0:T(8,128)}, f32[128,1024]{1,0:T(8,128)}, f32[32,576]{1,0:T(8,128)}) custom-call(s32[1,3]{1,0:T(1,128)} %keep_ref.1, bf16[32,576]{1,0:T(8,128)(2,1)} %lat_ref.1, bf16[128,2048]{1,0:T(8,128)(2,1)} %qn_hbm.1, bf16[128,1024]{1,0:T(8,128)(2,1)} %qr_hbm.1, bf16[128,2048]{1,0:T(8,128)(2,1)} %go_hbm.1, ...), custom_call_target="tpu_custom_call" | custom-call | tf_op jit(solution)/shard_map/latent_attention_grads/pallas_call | solution.py:394
  38.5 0.0 copy-start
  38.5 0.0 copy-start.1
  38.5 2.4 %copy.13 = f32[128,2048]{1,0:T(8,128)} copy(f32[128,2048]{1,0:T(8,128)} %get-tuple-element.6) | data formatting | bytes 2097152
  40.9 0.0 copy-done
  40.9 0.8 %copy.14 = f32[128,1024]{1,0:T(8,128)} copy(f32[128,1024]{1,0:T(8,128)S(1)} %copy-done) | data formatting | bytes 1048576
  41.6 0.0 copy-done.1
  41.7 0.6 %copy.15 = f32[32,576]{1,0:T(8,128)} copy(f32[32,576]{1,0:T(8,128)S(1)} %copy-done.1) | data formatting | bytes 147456
Async XLA Ops:
  38.5 2.4 %copy-start = (f32[128,1024]{1,0:T(8,128)S(1)}, f32[128,1024]{1,0:T(8,128)}, u32[]{:S(2)}) copy-start(f32[128,1024]{1,0:T(8,128)} %get-tuple-element.7) | copy-start | bytes 1572868
  38.5 3.2 %copy-start.1 = (f32[32,576]{1,0:T(8,128)S(1)}, f32[32,576]{1,0:T(8,128)}, u32[]{:S(2)}) copy-start(f32[32,576]{1,0:T(8,128)} %get-tuple-element.8) | copy-start | bytes 221188
where the time goes:
time: 42.5 us; the launch traced here: 42.3 us
  Pallas kernels  37.8 us (89%)
  local copies, waits for them, and re-layouts  3.79 us (9%)
  between operations  0.66 us (2%)
    pallas_call x1, Pallas kernels, on_device(): pl.pallas_call(functools.partial(kernel, n_ctx, n_head), out_shape=(jax.S...  37.8 us
    unnamed x7, local copies, waits for them, and re-layouts  3.79 us

commit v1 on v0

--- a/solution.py
+++ b/solution.py
@@ -30,10 +30,10 @@
 def kernel(
     n_ctx, n_head,
     keep_ref, lat_ref, qn_hbm, qr_hbm, go_hbm, ku_hbm, vu_hbm,
-    dqn_hbm, dqr_hbm, dlat_ref,
+    dqn, dqr, dlat_ref,
     win, qn, qr, go, ku, vu, krlo, krhi, bias, keys, vals, dkeys, dvals, slopes_grad,
-    rope_even, rope_odd, dqn, dqr, own, back, parts, got, zparts, zgot,
-    load_sem, store_sem, zs_sem, as_sem, bs_sem, cs_sem, win_sem,
+    rope_even, rope_odd, own, back, parts, got, zparts, zgot,
+    load_sem, zs_sem, as_sem, bs_sem, cs_sem, win_sem,
     ps_sem, got_sem, ws_sem, zgot_sem,
 ):
     c = lax.axis_index("ctx")
@@ -309,13 +309,6 @@
         return carry
 
     lax.fori_loop(0, heads // 2, dq_step, 0)
-    stores = [
-        pltpu.make_async_copy(dqn, dqn_hbm, store_sem.at[0]),
-        pltpu.make_async_copy(dqr, dqr_hbm, store_sem.at[1]),
-    ]
-    for store in stores:
-        store.start()
-
     own_ok = even | (c + 3 < n_ctx)
 
     def scatter(t):
@@ -376,8 +369,16 @@
         for t in range(n_head):
             part3(t).wait_send()
 
-    for store in stores:
-        store.wait()
+
+def write_out(a, b, c, a_hbm, b_hbm, c_hbm, sem):
+    copies = [
+        pltpu.make_async_copy(src, dst, sem.at[i])
+        for i, (src, dst) in enumerate([(a, a_hbm), (b, b_hbm), (c, c_hbm)])
+    ]
+    for copy in copies:
+        copy.start()
+    for copy in copies:
+        copy.wait()
 
 
 def on_device(n_ctx, n_head, query_nope, query_rope, grad_out, latent, key_up, value_up, block_keep):
@@ -391,15 +392,15 @@
     vmem, hbm = pl.BlockSpec(memory_space=pltpu.VMEM), pl.BlockSpec(memory_space=pl.ANY)
     dma = pltpu.SemaphoreType.DMA
     block = (n_head, rows, width)
-    return pl.pallas_call(
+    results = pl.pallas_call(
         functools.partial(kernel, n_ctx, n_head),
         out_shape=(
-            jax.ShapeDtypeStruct((group, wide), F32),
-            jax.ShapeDtypeStruct((group, rope_wide), F32),
-            jax.ShapeDtypeStruct((rows, width), F32),
+            pltpu.VMEM((group, wide), F32),
+            pltpu.VMEM((group, rope_wide), F32),
+            pltpu.VMEM((rows, width), F32),
         ),
         in_specs=[pl.BlockSpec(memory_space=pltpu.SMEM), vmem, hbm, hbm, hbm, hbm, hbm],
-        out_specs=(hbm, hbm, vmem),
+        out_specs=(vmem, vmem, vmem),
         scratch_shapes=[
             pltpu.VMEM((STEPS + 1,) + block, BF),
             pltpu.VMEM((group, wide), BF),
@@ -417,8 +418,6 @@
             pltpu.VMEM((heads, span, group), BF),
             pltpu.VMEM((span, 2 * ROPE), F32),
             pltpu.VMEM((span, 2 * ROPE), F32),
-            pltpu.VMEM((group, wide), F32),
-            pltpu.VMEM((group, rope_wide), F32),
             pltpu.VMEM(block, F32),
             pltpu.VMEM(block, F32),
             pltpu.VMEM((3,) + block, BF),
@@ -426,7 +425,6 @@
             pltpu.VMEM(block, BF),
             pltpu.VMEM(block, BF),
             dma((5,)),
-            dma((2,)),
             dma((n_head,)),
             dma((n_head,)),
             dma((n_head,)),
@@ -440,6 +438,15 @@
         compiler_params=pltpu.CompilerParams(collective_id=0, has_side_effects=True),
         name="latent_attention_grads",
     )(block_keep, latent, query_nope, query_rope, grad_out, key_up, value_up)
+
+    return pl.pallas_call(
+        write_out,
+        out_shape=tuple(jax.ShapeDtypeStruct(r.shape, r.dtype) for r in results),
+        in_specs=[vmem] * 3,
+        out_specs=[hbm] * 3,
+        scratch_shapes=[dma((3,))],
+        name="write_out",
+    )(*(pltpu.with_memory_space_constraint(r, pltpu.VMEM) for r in results))
 
 
 def solution(mesh):

time: 42.5 us -> 39.2 us (0.922)
  local copies, waits for them, and re-layouts: 3.79 us -> 0 us
  Pallas kernels: 37.8 us -> 38.4 us
    unnamed x7 -> x0, local copies, waits for them, and re-layouts: 3.79 us -> none
    pallas_call x1 -> x2, Pallas kernels: 37.8 us -> 38.4 us  [the longest x1 37.2 us: on_device(): pl.pallas_call(functools.partial(kernel, n_ctx, n_head), out_shape=(pltpu...]
where the time goes in v1:
time: 39.2 us; the launch traced here: 39 us
  Pallas kernels  38.4 us (98%)
  between operations  0.64 us (2%)
    pallas_call x1, Pallas kernels, on_device(): pl.pallas_call(functools.partial(kernel, n_ctx, n_head), out_shape=(pltpu...  37.2 us
    pallas_call x1, Pallas kernels, on_device(): pl.pallas_call(write_out, out_shape=tuple((jax.ShapeDtypeStruct(r.shape,...  1.18 us

profile of v1, /device:TPU:0, one launch (start us, length us, event | category | flops | bytes accessed | tf_op | source)
XLA Modules:
  0.0 39.0 jit_solution(15274116663841716241)
XLA Ops:
  0.6 37.2 %latent_attention_grads.1 = (f32[128,2048]{1,0:T(8,128)S(1)}, f32[128,1024]{1,0:T(8,128)S(1)}, f32[32,576]{1,0:T(8,128)S(1)}) custom-call(s32[1,3]{1,0:T(1,128)} %keep_ref.1, bf16[32,576]{1,0:T(8,128)(2,1)} %lat_ref.1, bf16[128,2048]{1,0:T(8,128)(2,1)} %qn_hbm.1, bf16[128,1024]{1,0:T(8,128)(2,1)} %qr_hbm.1, bf16[128,2048]{1,0:T(8,128)(2,1)} %go_hbm.1, ...), custom_call_target="tpu_custom_call" | custom-call | tf_op jit(solution)/shard_map/latent_attention_grads/pallas_call | solution.py:395
  37.8 1.2 %write_out.1 = (f32[128,2048]{1,0:T(8,128)}, f32[128,1024]{1,0:T(8,128)}, f32[32,576]{1,0:T(8,128)}) custom-call(f32[128,2048]{1,0:T(8,128)S(1)} %get-tuple-element.6.a, f32[128,1024]{1,0:T(8,128)S(1)} %get-tuple-element.7.b, f32[32,576]{1,0:T(8,128)S(1)} %get-tuple-element.8.c), custom_call_target="tpu_custom_call" | custom-call | tf_op jit(solution)/shard_map/write_out/pallas_call | solution.py:442

commit v2 on v1

v2 whole, which is shorter than its diff:
```python
import functools
import math

import jax
import jax.numpy as jnp
from jax import lax
from jax.experimental import pallas as pl
from jax.experimental.pallas import tpu as pltpu
from jax.sharding import PartitionSpec as P

NOPE = 128
ROPE = 64
VDIM = 128
RANK = 512
STEPS = 3
BF = jnp.bfloat16
F32 = jnp.float32
MESH = pl.DeviceIdType.MESH
FOR_BACK, FOR_OWN, FROM_NEXT = 0, 1, 2


def dot_nt(a, b):
    return lax.dot_general(a, b, (((1,), (1,)), ((), ())), preferred_element_type=F32)


def dot_tn(a, b):
    return lax.dot_general(a, b, (((0,), (0,)), ((), ())), preferred_element_type=F32)


def two_heads(pair):
    width = pair.shape[1] // 2
    zero = jnp.zeros((pair.shape[0], width), pair.dtype)
    first = jnp.concatenate([pair[:, :width], zero], axis=1)
    second = jnp.concatenate([zero, pair[:, width:]], axis=1)
    return jnp.concatenate([first, second], axis=0)


def kernel(
    n_ctx, n_head,
    keep_hbm, lat_hbm, qn_hbm, qr_hbm, go_hbm, ku_hbm, vu_hbm,
    dqn, dqr, dlat_ref,
    keep, win, qn, qr, go, ku, vu, kut, vut, qrs, krlo, krhi, bias, keys, vals, dkeys, dvals, slopes_grad,
    raw, tops, slopes, weights, own, back, parts, got, zparts, zgot,
    load_sem, lat_sem, keep_sem, zs_sem, as_sem, bs_sem, cs_sem, win_sem,
    ps_sem, got_sem, ws_sem, zgot_sem,
):
    c = lax.axis_index("ctx")
    h = lax.axis_index("head")
    even = lax.rem(c, 2) == 0
    partner = jnp.where(even, c + 1, c - 1)
    far = jnp.where(even, c - 3, c + 3)
    has_far = (far >= 0) & (far < n_ctx)
    rows = lat_hbm.shape[0]
    group = rows * n_head
    span = group * (STEPS + 1)
    heads = qn.shape[1] // NOPE
    scale = 1.0 / math.sqrt(NOPE + ROPE)

    loads = [
        pltpu.make_async_copy(src, dst, load_sem.at[i])
        for i, (src, dst) in enumerate(
            [(ku_hbm, ku), (vu_hbm, vu), (qn_hbm, qn), (qr_hbm, qr), (go_hbm, go)]
        )
    ]
    barrier = pltpu.get_barrier_semaphore()
    for t in range(1, n_head):
        pl.semaphore_signal(
            barrier, inc=1, device_id=(c, lax.rem(h + t, n_head)), device_id_type=MESH
        )
    pl.semaphore_signal(barrier, inc=1, device_id=(partner, h), device_id_type=MESH)
    for ok, who in ((c >= 2, c - 2), (c + 2 < n_ctx, c + 2), (has_far, far)):

        @pl.when(ok)
        def _():
            pl.semaphore_signal(barrier, inc=1, device_id=(who, h), device_id_type=MESH)

    own_copy = pltpu.make_async_copy(lat_hbm, win.at[3, h], lat_sem)
    own_copy.start()
    keep_copy = pltpu.make_async_copy(keep_hbm, keep, keep_sem)
    keep_copy.start()
    for load in loads:
        load.start()

    peers = n_head
    for ok in (c >= 2, c + 2 < n_ctx, has_far):
        peers = peers + jnp.where(ok, 1, 0)
    key_at = lax.broadcasted_iota(jnp.int32, (group, group), 0)
    query_at = lax.broadcasted_iota(jnp.int32, (group, group), 1)
    bias[...] = jnp.where(key_at <= query_at, 0.0, -jnp.inf).astype(F32)
    keep_copy.wait()
    flags = [None] * STEPS
    for k in range(1, STEPS + 1):
        flags[STEPS - k] = jnp.where((keep[0, k - 1] == 1) & (c >= k), 0.0, -jnp.inf).astype(F32)

        @pl.when(c < k)
        def _():
            win[STEPS - k] = jnp.zeros(win.shape[1:], BF)

    def at_pair(j, width):
        return pl.ds(pl.multiple_of(j * width, width), width)

    def transpose(src, dst):
        def step(j, carry):
            dst[at_pair(j, 2 * NOPE), :] = src[:, at_pair(j, 2 * NOPE)].T
            return carry

        lax.fori_loop(0, heads // 2, step, 0, unroll=2)

    loads[0].wait()
    transpose(ku, kut)
    pl.semaphore_wait(barrier, peers)
    own_copy.wait()

    before, after = h, n_head - 1 - h
    twice = 2 * jnp.minimum(before, after)

    def near(t):
        if t == 0:
            return h
        both = h - (t + 1) // 2 if t % 2 else h + t // 2
        rest = t - jnp.minimum(before, after)
        return jnp.where(t <= twice, both, jnp.where(before < after, h + rest, h - rest))

    piece = near

    def over_head(t):
        return pltpu.make_async_remote_copy(
            src_ref=win.at[3, h], dst_ref=win.at[3, h], send_sem=zs_sem.at[t],
            recv_sem=win_sem.at[3, h], device_id=(c, near(t)), device_id_type=MESH,
        )

    def own_source(t):
        return win.at[3, piece(t)]

    def send_two_ahead(t):
        return pltpu.make_async_remote_copy(
            src_ref=own_source(t), dst_ref=win.at[1, piece(t)], send_sem=as_sem.at[t],
            recv_sem=win_sem.at[1, piece(t)], device_id=(c + 2, h), device_id_type=MESH,
        )

    b_slot = jnp.where(even, 2, 0)
    b_who = jnp.where(even, c + 1, c + 3)
    b_ok = b_who < n_ctx

    def send_odd_ahead(t):
        return pltpu.make_async_remote_copy(
            src_ref=own_source(t), dst_ref=win.at[b_slot, piece(t)], send_sem=bs_sem.at[t],
            recv_sem=win_sem.at[b_slot, piece(t)], device_id=(b_who, h), device_id_type=MESH,
        )

    c_slot = jnp.where(even, 0, 2)

    def forward(t):
        return pltpu.make_async_remote_copy(
            src_ref=win.at[1, piece(t)], dst_ref=win.at[c_slot, piece(t)], send_sem=cs_sem.at[t],
            recv_sem=win_sem.at[c_slot, piece(t)], device_id=(partner, h), device_id_type=MESH,
        )

    def wait_piece(slot, t):
        pltpu.make_async_remote_copy(
            src_ref=win.at[3, h], dst_ref=win.at[slot, piece(t)], send_sem=zs_sem.at[0],
            recv_sem=win_sem.at[slot, piece(t)], device_id=(partner, h), device_id_type=MESH,
        ).wait_recv()

    @pl.when(c + 2 < n_ctx)
    def _():
        send_two_ahead(0).start()

    for t in range(1, n_head):
        over_head(n_head - t).start()

    @pl.when(b_ok)
    def _():
        send_odd_ahead(0).start()

    for load in loads[1:]:
        load.wait()
    transpose(vu, vut)

    low_half = lax.broadcasted_iota(jnp.int32, (group, 2 * ROPE), 1) < ROPE

    def stack_step(j, carry):
        pair = qr[:, at_pair(j, 2 * ROPE)]
        for e, mine in enumerate((low_half, jnp.logical_not(low_half))):
            at = pl.ds(pl.multiple_of((2 * j + e) * group, group), group)
            qrs[at, :] = jnp.where(mine, pair, jnp.zeros_like(pair))
        return carry

    lax.fori_loop(0, heads // 2, stack_step, 0, unroll=2)

    for t in range(1, n_head):
        wait_piece(3, t)

        @pl.when(c + 2 < n_ctx)
        def _():
            send_two_ahead(t).start()

        @pl.when(b_ok)
        def _():
            send_odd_ahead(t).start()

    def expand(slot):
        content = win[slot, :, :, :RANK].reshape(group, RANK)
        rope_keys = win[slot, :, :, RANK:].reshape(group, ROPE)
        pad = jnp.zeros((group, ROPE), BF)
        at = pl.ds(pl.multiple_of(slot * group, group), group)
        krlo[at, :] = jnp.concatenate([rope_keys, pad], axis=1)
        krhi[at, :] = jnp.concatenate([pad, rope_keys], axis=1)

        def expand_step(j, carry):
            lanes = at_pair(j, 2 * NOPE)
            keys[at, lanes] = jnp.dot(content, ku[:, lanes], preferred_element_type=F32).astype(BF)
            vals[at, lanes] = jnp.dot(content, vu[:, lanes], preferred_element_type=F32).astype(BF)
            return carry

        lax.fori_loop(0, heads // 2, expand_step, 0, unroll=heads // 2)

    def take(slot, passing_on=False):
        @pl.when(c >= STEPS - slot)
        def _():
            for t in range(n_head):
                wait_piece(slot, t)
                if passing_on:
                    forward(t).start()

        expand(slot)

    expand(STEPS)
    take(jnp.where(even, 0, 2))
    take(1, True)
    take(jnp.where(even, 2, 0))

    pairs = heads // 2
    rate = scale * math.log2(math.e)
    blocks = [slice(i * group, (i + 1) * group) for i in range(STEPS + 1)]

    def fold(value, how):
        return how(value.reshape(group // 8, 8, group), axis=0)

    def lanes_of(e):
        return slice(e * NOPE, (e + 1) * NOPE)

    def score_pair(j, at):
        wide = at_pair(j, 2 * NOPE)
        key_pair = keys[:, wide]
        qn_pair = qn[:, wide]
        qr_pair = qr[:, at_pair(j, 2 * ROPE)]
        for e, kr in enumerate((krlo, krhi)):
            key = jnp.concatenate([key_pair[:, lanes_of(e)], kr[...]], axis=1)
            query = jnp.concatenate([qn_pair[:, lanes_of(e)], qr_pair], axis=1)
            scores = dot_nt(key, query)
            top = None
            for i, block in enumerate(blocks):
                piece = scores[block]
                if i == STEPS:
                    piece = piece + bias[...]
                raw[at, block, lanes_of(e)] = piece
                high = fold(piece, jnp.max)
                if i < STEPS:
                    high = high + flags[i]
                top = high if top is None else jnp.maximum(top, high)
            tops[at, :, lanes_of(e)] = jnp.broadcast_to(jnp.max(top, axis=0, keepdims=True), (8, group))
        slopes[at] = dot_nt(vals[:, wide], two_heads(go[:, wide]))

    def softmax_pair(j, at):
        for e in range(2):
            lanes = lanes_of(e)
            top = tops[at, 0:1, lanes] * rate
            shift = [top - flags[i] if i < STEPS else top for i in range(STEPS + 1)]
            total = None
            for i, block in enumerate(blocks):
                part = fold(jnp.exp2(raw[at, block, lanes] * rate - shift[i]), jnp.sum)
                total = part if total is None else total + part
            norm = jnp.log2(jnp.sum(total, axis=0, keepdims=True))
            delta = None
            for i, block in enumerate(blocks):
                probs = jnp.exp2(raw[at, block, lanes] * rate - (shift[i] + norm))
                weights[at, block, lanes] = probs.astype(BF)
                part = fold(probs * slopes[at, block, lanes], jnp.sum)
                delta = part if delta is None else delta + part
            delta = jnp.sum(delta, axis=0, keepdims=True)
            mine = at_pair(2 * j + e, group)
            for block in blocks:
                slope = ((slopes[at, block, lanes] - delta) * scale).astype(BF)
                slopes_grad[block, mine] = weights[at, block, lanes] * slope

    def grad_pair(j, at):
        wide = at_pair(j, 2 * NOPE)
        grad = slopes_grad[:, at_pair(j, 2 * group)]
        dkeys[:, wide] = jnp.dot(grad, two_heads(qn[:, wide]), preferred_element_type=F32).astype(BF)
        dvals[:, wide] = jnp.dot(weights[at], two_heads(go[:, wide]), preferred_element_type=F32).astype(BF)

    score_pair(0, 0)
    score_pair(1, 1)
    softmax_pair(0, 0)

    def pair_step(j, carry):
        now = lax.rem(j, 2)
        grad_pair(j - 1, 1 - now)
        score_pair(j + 1, 1 - now)
        softmax_pair(j, now)
        return carry

    lax.fori_loop(1, pairs - 1, pair_step, 0, unroll=min(6, pairs - 2))
    last = (pairs - 1) % 2
    grad_pair(pairs - 2, 1 - last)
    softmax_pair(pairs - 1, last)
    grad_pair(pairs - 1, last)

    def terms_of(k):
        at = pl.ds(pl.multiple_of((STEPS - k) * group, group), group)
        content = jnp.dot(dkeys[at, :], kut[...], preferred_element_type=F32)
        content = content + jnp.dot(dvals[at, :], vut[...], preferred_element_type=F32)
        both = jnp.dot(slopes_grad[at, :], qrs[...], preferred_element_type=F32)
        rope = both[:, :ROPE] + both[:, ROPE:]
        return content.reshape(n_head, rows, RANK), rope.reshape(n_head, rows, ROPE)

    def put(ref, k):
        content, rope = terms_of(k)
        ref[:, :, :RANK] = content.astype(ref.dtype)
        ref[:, :, RANK:] = rope.astype(ref.dtype)

    order = [*range(n_head - 1, 0, -1), 0]
    chunk = near
    back_k, own_k = jnp.where(even, 1, 3), jnp.where(even, 3, 1)
    far_who = jnp.where(even, c - 3, c - 1)

    def send_part(i, slot, who, t):
        return pltpu.make_async_remote_copy(
            src_ref=parts.at[i, chunk(t)], dst_ref=got.at[slot, chunk(t)], send_sem=ps_sem.at[i, t],
            recv_sem=got_sem.at[slot, chunk(t)], device_id=(who, h), device_id_type=MESH,
        )

    def part_back(t):
        return send_part(0, FOR_BACK, partner, t)

    def part_next(t):
        return send_part(2, FROM_NEXT, c - 2, t)

    def part_own(t):
        return send_part(1, FOR_OWN, far_who, t)

    def wait_part(slot, t):
        send_part(0, slot, partner, t).wait_recv()

    def put_own_part():
        put(parts.at[1], own_k)

        @pl.when(c >= own_k)
        def _():
            for t in order:
                part_own(t).start()

    own_first = (lax.rem(c, 4) == 2) & (c >= own_k)
    pl.when(own_first)(put_own_part)

    put(parts.at[0], back_k)

    @pl.when(c >= back_k)
    def _():
        for t in order:
            part_back(t).start()

    put(back, 2)

    @pl.when(c >= 2)
    def _():
        for t in order:
            wait_part(FOR_BACK, t)
            parts[2, chunk(t)] = (back[chunk(t)] + got[FOR_BACK, chunk(t)].astype(F32)).astype(BF)
            part_next(t).start()

    pl.when(jnp.logical_not(own_first))(put_own_part)

    put(own, 0)

    def dq_step(j, carry):
        wide = at_pair(j, 2 * NOPE)
        key_pair = keys[:, wide]
        nope, rope = [], None
        for e, kr in enumerate((krlo, krhi)):
            key = jnp.concatenate([key_pair[:, e * NOPE : (e + 1) * NOPE], kr[...]], axis=1)
            both = dot_tn(slopes_grad[:, at_pair(2 * j + e, group)], key)
            nope.append(both[:, :NOPE])
            rope = both[:, NOPE:] if rope is None else rope + both[:, NOPE:]
        dqn[:, wide] = jnp.concatenate(nope, axis=1)
        dqr[:, at_pair(j, 2 * ROPE)] = rope
        return carry

    lax.fori_loop(0, heads // 2, dq_step, 0, unroll=2)
    own_ok = even | (c + 3 < n_ctx)

    def scatter(t):
        return pltpu.make_async_remote_copy(
            src_ref=zparts.at[chunk(t)], dst_ref=zgot.at[h], send_sem=ws_sem.at[t],
            recv_sem=zgot_sem.at[h], device_id=(c, chunk(t)), device_id_type=MESH,
        )

    for t in order:

        @pl.when(own_ok)
        def _():
            wait_part(FOR_OWN, t)
            own[chunk(t)] += got[FOR_OWN, chunk(t)].astype(F32)

        @pl.when(c + 2 < n_ctx)
        def _():
            wait_part(FROM_NEXT, t)
            own[chunk(t)] += got[FROM_NEXT, chunk(t)].astype(F32)

        if t > 0:
            zparts[chunk(t)] = own[chunk(t)].astype(BF)
            scatter(t).start()

    total = own[h]
    for t in range(1, n_head):
        pltpu.make_async_remote_copy(
            src_ref=zparts.at[h], dst_ref=zgot.at[near(t)], send_sem=ws_sem.at[t],
            recv_sem=zgot_sem.at[near(t)], device_id=(c, near(t)), device_id_type=MESH,
        ).wait_recv()
        total = total + zgot[near(t)].astype(F32)
    dlat_ref[...] = total

    for t in range(1, n_head):
        scatter(t).wait_send()
        over_head(t).wait_send()

    @pl.when(c + 2 < n_ctx)
    def _():
        for t in range(n_head):
            send_two_ahead(t).wait_send()

    @pl.when(b_ok)
    def _():
        for t in range(n_head):
            send_odd_ahead(t).wait_send()

    @pl.when(c >= 2)
    def _():
        for t in range(n_head):
            forward(t).wait_send()
            part_next(t).wait_send()

    @pl.when(c >= back_k)
    def _():
        for t in range(n_head):
            part_back(t).wait_send()

    @pl.when(c >= own_k)
    def _():
        for t in range(n_head):
            part_own(t).wait_send()


def write_out(a, b, c, a_hbm, b_hbm, c_hbm, sem):
    copies = [
        pltpu.make_async_copy(src, dst, sem.at[i])
        for i, (src, dst) in enumerate([(a, a_hbm), (b, b_hbm), (c, c_hbm)])
    ]
    for copy in copies:
        copy.start()
    for copy in copies:
        copy.wait()


def on_device(n_ctx, n_head, query_nope, query_rope, grad_out, latent, key_up, value_up, block_keep):
    rows, width = latent.shape
    group = query_nope.shape[0]
    span = group * (STEPS + 1)
    wide = query_nope.shape[1]
    rope_wide = query_rope.shape[1]
    heads = wide // NOPE
    assert block_keep.shape[1] == STEPS and n_ctx % 2 == 0 and heads % 2 == 0 and heads >= 4
    vmem, hbm = pl.BlockSpec(memory_space=pltpu.VMEM), pl.BlockSpec(memory_space=pl.ANY)
    dma = pltpu.SemaphoreType.DMA
    block = (n_head, rows, width)
    results = pl.pallas_call(
        functools.partial(kernel, n_ctx, n_head),
        out_shape=(
            pltpu.VMEM((group, wide), F32),
            pltpu.VMEM((group, rope_wide), F32),
            pltpu.VMEM((rows, width), F32),
        ),
        in_specs=[hbm, hbm, hbm, hbm, hbm, hbm, hbm],
        out_specs=(vmem, vmem, vmem),
        scratch_shapes=[
            pltpu.SMEM(block_keep.shape, block_keep.dtype),
            pltpu.VMEM((STEPS + 1,) + block, BF),
            pltpu.VMEM((group, wide), BF),
            pltpu.VMEM((group, rope_wide), BF),
            pltpu.VMEM((group, wide), BF),
            pltpu.VMEM((RANK, wide), BF),
            pltpu.VMEM((RANK, wide), BF),
            pltpu.VMEM((wide, RANK), BF),
            pltpu.VMEM((wide, RANK), BF),
            pltpu.VMEM((heads * group, 2 * ROPE), BF),
            pltpu.VMEM((span, 2 * ROPE), BF),
            pltpu.VMEM((span, 2 * ROPE), BF),
            pltpu.VMEM((group, group), F32),
            pltpu.VMEM((span, wide), BF),
            pltpu.VMEM((span, wide), BF),
            pltpu.VMEM((span, wide), BF),
            pltpu.VMEM((span, wide), BF),
            pltpu.VMEM((span, heads * group), BF),
            pltpu.VMEM((2, span, 2 * group), F32),
            pltpu.VMEM((2, 8, 2 * group), F32),
            pltpu.VMEM((2, span, 2 * group), F32),
            pltpu.VMEM((2, span, 2 * group), BF),
            pltpu.VMEM(block, F32),
            pltpu.VMEM(block, F32),
            pltpu.VMEM((3,) + block, BF),
            pltpu.VMEM((3,) + block, BF),
            pltpu.VMEM(block, BF),
            pltpu.VMEM(block, BF),
            dma((5,)),
            dma(()),
            dma(()),
            dma((n_head,)),
            dma((n_head,)),
            dma((n_head,)),
            dma((n_head,)),
            dma((STEPS + 1, n_head)),
            dma((3, n_head)),
            dma((3, n_head)),
            dma((n_head,)),
            dma((n_head,)),
        ],
        compiler_params=pltpu.CompilerParams(collective_id=0, has_side_effects=True),
        name="latent_attention_grads",
    )(block_keep, latent, query_nope, query_rope, grad_out, key_up, value_up)

    return pl.pallas_call(
        write_out,
        out_shape=tuple(jax.ShapeDtypeStruct(r.shape, r.dtype) for r in results),
        in_specs=[vmem] * 3,
        out_specs=[hbm] * 3,
        scratch_shapes=[dma((3,))],
        name="write_out",
    )(*(pltpu.with_memory_space_constraint(r, pltpu.VMEM) for r in results))


def solution(mesh):
    placed = (
        P("ctx", "head"),
        P("ctx", "head"),
        P("ctx", "head"),
        P(("ctx", "head"), None),
        P(None, "head"),
        P(None, "head"),
        P("ctx", None),
    )
    return jax.shard_map(
        functools.partial(on_device, mesh.shape["ctx"], mesh.shape["head"]),
        mesh=mesh,
        in_specs=placed,
        out_specs=(P("ctx", "head"), P("ctx", "head"), P(("ctx", "head"), None)),
        check_vma=False,
    )
```

time: 39.2 us -> 33.9 us (0.86)
  Pallas kernels: 38.4 us -> 33.2 us
    pallas_call x1, Pallas kernels: 37.2 us -> 32 us  [on_device(): pl.pallas_call(functools.partial(kernel, n_ctx, n_head), out_shape=(pltpu...]
where the time goes in v2:
time: 33.9 us; the launch traced here: 33.8 us
  Pallas kernels  33.2 us (98%)
  between operations  0.64 us (2%)
    pallas_call x1, Pallas kernels, on_device(): pl.pallas_call(functools.partial(kernel, n_ctx, n_head), out_shape=(pltpu...  32 us
    pallas_call x1, Pallas kernels, on_device(): pl.pallas_call(write_out, out_shape=tuple((jax.ShapeDtypeStruct(r.shape,...  1.18 us

profile of v2, /device:TPU:0, one launch (start us, length us, event | category | flops | bytes accessed | tf_op | source)
XLA Modules:
  0.0 33.8 jit_solution(1215336127220237275)
XLA Ops:
  0.6 32.0 %latent_attention_grads.1 = (f32[128,2048]{1,0:T(8,128)S(1)}, f32[128,1024]{1,0:T(8,128)S(1)}, f32[32,576]{1,0:T(8,128)S(1)}) custom-call(s32[1,3]{1,0:T(1,128)} %keep_hbm.1, bf16[32,576]{1,0:T(8,128)(2,1)} %lat_hbm.1, bf16[128,2048]{1,0:T(8,128)(2,1)} %qn_hbm.1, bf16[128,1024]{1,0:T(8,128)(2,1)} %qr_hbm.1, bf16[128,2048]{1,0:T(8,128)(2,1)} %go_hbm.1, ...), custom_call_target="tpu_custom_call" | custom-call | tf_op jit(solution)/shard_map/latent_attention_grads/pallas_call | solution.py:477
  32.6 1.2 %write_out.1 = (f32[128,2048]{1,0:T(8,128)}, f32[128,1024]{1,0:T(8,128)}, f32[32,576]{1,0:T(8,128)}) custom-call(f32[128,2048]{1,0:T(8,128)S(1)} %get-tuple-element.6.a, f32[128,1024]{1,0:T(8,128)S(1)} %get-tuple-element.7.b, f32[32,576]{1,0:T(8,128)S(1)} %get-tuple-element.8.c), custom_call_target="tpu_custom_call" | custom-call | tf_op jit(solution)/shard_map/write_out/pallas_call | solution.py:532

commit v3 on v2

--- a/solution.py
+++ b/solution.py
@@ -41,15 +41,13 @@
     dqn, dqr, dlat_ref,
     keep, win, qn, qr, go, ku, vu, kut, vut, qrs, krlo, krhi, bias, keys, vals, dkeys, dvals, slopes_grad,
     raw, tops, slopes, weights, own, back, parts, got, zparts, zgot,
-    load_sem, lat_sem, keep_sem, zs_sem, as_sem, bs_sem, cs_sem, win_sem,
+    load_sem, lat_sem, keep_sem, zs_sem, as_sem, bs_sem, cs_sem, ds_sem, win_sem,
     ps_sem, got_sem, ws_sem, zgot_sem,
 ):
     c = lax.axis_index("ctx")
     h = lax.axis_index("head")
     even = lax.rem(c, 2) == 0
     partner = jnp.where(even, c + 1, c - 1)
-    far = jnp.where(even, c - 3, c + 3)
-    has_far = (far >= 0) & (far < n_ctx)
     rows = lat_hbm.shape[0]
     group = rows * n_head
     span = group * (STEPS + 1)
@@ -68,7 +66,7 @@
             barrier, inc=1, device_id=(c, lax.rem(h + t, n_head)), device_id_type=MESH
         )
     pl.semaphore_signal(barrier, inc=1, device_id=(partner, h), device_id_type=MESH)
-    for ok, who in ((c >= 2, c - 2), (c + 2 < n_ctx, c + 2), (has_far, far)):
+    for ok, who in ((c >= 2, c - 2), (c + 2 < n_ctx, c + 2), (c >= 3, c - 3), (c + 3 < n_ctx, c + 3)):
 
         @pl.when(ok)
         def _():
@@ -82,7 +80,7 @@
         load.start()
 
     peers = n_head
-    for ok in (c >= 2, c + 2 < n_ctx, has_far):
+    for ok in (c >= 2, c + 2 < n_ctx, c >= 3, c + 3 < n_ctx):
         peers = peers + jnp.where(ok, 1, 0)
     key_at = lax.broadcasted_iota(jnp.int32, (group, group), 0)
     query_at = lax.broadcasted_iota(jnp.int32, (group, group), 1)
@@ -125,7 +123,7 @@
 
     def over_head(t):
         return pltpu.make_async_remote_copy(
-            src_ref=win.at[3, h], dst_ref=win.at[3, h], send_sem=zs_sem.at[t],
+            src_ref=win.at[3, h], dst_ref=win.at[3, h], send_sem=zs_sem,
             recv_sem=win_sem.at[3, h], device_id=(c, near(t)), device_id_type=MESH,
         )
 
@@ -134,7 +132,7 @@
 
     def send_two_ahead(t):
         return pltpu.make_async_remote_copy(
-            src_ref=own_source(t), dst_ref=win.at[1, piece(t)], send_sem=as_sem.at[t],
+            src_ref=own_source(t), dst_ref=win.at[1, piece(t)], send_sem=as_sem,
             recv_sem=win_sem.at[1, piece(t)], device_id=(c + 2, h), device_id_type=MESH,
         )
 
@@ -144,21 +142,30 @@
 
     def send_odd_ahead(t):
         return pltpu.make_async_remote_copy(
-            src_ref=own_source(t), dst_ref=win.at[b_slot, piece(t)], send_sem=bs_sem.at[t],
+            src_ref=own_source(t), dst_ref=win.at[b_slot, piece(t)], send_sem=bs_sem,
             recv_sem=win_sem.at[b_slot, piece(t)], device_id=(b_who, h), device_id_type=MESH,
         )
 
     c_slot = jnp.where(even, 0, 2)
 
+    late = n_head // 2
+    direct_ok = even & (c + 3 < n_ctx)
+
+    def send_direct(t):
+        return pltpu.make_async_remote_copy(
+            src_ref=own_source(t), dst_ref=win.at[0, piece(t)], send_sem=ds_sem,
+            recv_sem=win_sem.at[0, piece(t)], device_id=(c + 3, h), device_id_type=MESH,
+        )
+
     def forward(t):
         return pltpu.make_async_remote_copy(
-            src_ref=win.at[1, piece(t)], dst_ref=win.at[c_slot, piece(t)], send_sem=cs_sem.at[t],
+            src_ref=win.at[1, piece(t)], dst_ref=win.at[c_slot, piece(t)], send_sem=cs_sem,
             recv_sem=win_sem.at[c_slot, piece(t)], device_id=(partner, h), device_id_type=MESH,
         )
 
     def wait_piece(slot, t):
         pltpu.make_async_remote_copy(
-            src_ref=win.at[3, h], dst_ref=win.at[slot, piece(t)], send_sem=zs_sem.at[0],
+            src_ref=win.at[3, h], dst_ref=win.at[slot, piece(t)], send_sem=zs_sem,
             recv_sem=win_sem.at[slot, piece(t)], device_id=(partner, h), device_id_type=MESH,
         ).wait_recv()
 
@@ -194,6 +201,12 @@
         @pl.when(c + 2 < n_ctx)
         def _():
             send_two_ahead(t).start()
+
+        if t >= late:
+
+            @pl.when(direct_ok)
+            def _():
+                send_direct(t).start()
 
         @pl.when(b_ok)
         def _():
@@ -220,8 +233,13 @@
         def _():
             for t in range(n_head):
                 wait_piece(slot, t)
-                if passing_on:
+                if passing_on and t < late:
                     forward(t).start()
+                elif passing_on:
+
+                    @pl.when(jnp.logical_not(even))
+                    def _():
+                        forward(t).start()
 
         expand(slot)
 
@@ -245,6 +263,7 @@
         key_pair = keys[:, wide]
         qn_pair = qn[:, wide]
         qr_pair = qr[:, at_pair(j, 2 * ROPE)]
+        slopes[at] = dot_nt(vals[:, wide], two_heads(go[:, wide]))
         for e, kr in enumerate((krlo, krhi)):
             key = jnp.concatenate([key_pair[:, lanes_of(e)], kr[...]], axis=1)
             query = jnp.concatenate([qn_pair[:, lanes_of(e)], qr_pair], axis=1)
@@ -260,11 +279,11 @@
                     high = high + flags[i]
                 top = high if top is None else jnp.maximum(top, high)
             tops[at, :, lanes_of(e)] = jnp.broadcast_to(jnp.max(top, axis=0, keepdims=True), (8, group))
-        slopes[at] = dot_nt(vals[:, wide], two_heads(go[:, wide]))
 
     def softmax_pair(j, at):
         for e in range(2):
             lanes = lanes_of(e)
+            mine = at_pair(2 * j + e, group)
             top = tops[at, 0:1, lanes] * rate
             shift = [top - flags[i] if i < STEPS else top for i in range(STEPS + 1)]
             total = None
@@ -275,20 +294,13 @@
             delta = None
             for i, block in enumerate(blocks):
                 probs = jnp.exp2(raw[at, block, lanes] * rate - (shift[i] + norm))
-                weights[at, block, lanes] = probs.astype(BF)
+                weights[block, mine] = probs.astype(BF)
                 part = fold(probs * slopes[at, block, lanes], jnp.sum)
                 delta = part if delta is None else delta + part
             delta = jnp.sum(delta, axis=0, keepdims=True)
-            mine = at_pair(2 * j + e, group)
             for block in blocks:
                 slope = ((slopes[at, block, lanes] - delta) * scale).astype(BF)
-                slopes_grad[block, mine] = weights[at, block, lanes] * slope
-
-    def grad_pair(j, at):
-        wide = at_pair(j, 2 * NOPE)
-        grad = slopes_grad[:, at_pair(j, 2 * group)]
-        dkeys[:, wide] = jnp.dot(grad, two_heads(qn[:, wide]), preferred_element_type=F32).astype(BF)
-        dvals[:, wide] = jnp.dot(weights[at], two_heads(go[:, wide]), preferred_element_type=F32).astype(BF)
+                slopes_grad[block, mine] = weights[block, mine] * slope
 
     score_pair(0, 0)
     score_pair(1, 1)
@@ -296,21 +308,27 @@
 
     def pair_step(j, carry):
         now = lax.rem(j, 2)
-        grad_pair(j - 1, 1 - now)
         score_pair(j + 1, 1 - now)
         softmax_pair(j, now)
         return carry
 
     lax.fori_loop(1, pairs - 1, pair_step, 0, unroll=min(6, pairs - 2))
     last = (pairs - 1) % 2
-    grad_pair(pairs - 2, 1 - last)
     softmax_pair(pairs - 1, last)
-    grad_pair(pairs - 1, last)
 
     def terms_of(k):
         at = pl.ds(pl.multiple_of((STEPS - k) * group, group), group)
-        content = jnp.dot(dkeys[at, :], kut[...], preferred_element_type=F32)
-        content = content + jnp.dot(dvals[at, :], vut[...], preferred_element_type=F32)
+        for j in range(pairs):
+            mine = slice(j * 2 * group, (j + 1) * 2 * group)
+            wide = slice(j * 2 * NOPE, (j + 1) * 2 * NOPE)
+            dkeys[:, wide] = jnp.dot(
+                slopes_grad[at, mine], two_heads(qn[:, wide]), preferred_element_type=F32
+            ).astype(BF)
+            dvals[:, wide] = jnp.dot(
+                weights[at, mine], two_heads(go[:, wide]), preferred_element_type=F32
+            ).astype(BF)
+        content = jnp.dot(dkeys[...], kut[...], preferred_element_type=F32)
+        content = content + jnp.dot(dvals[...], vut[...], preferred_element_type=F32)
         both = jnp.dot(slopes_grad[at, :], qrs[...], preferred_element_type=F32)
         rope = both[:, :ROPE] + both[:, ROPE:]
         return content.reshape(n_head, rows, RANK), rope.reshape(n_head, rows, ROPE)
@@ -327,7 +345,7 @@
 
     def send_part(i, slot, who, t):
         return pltpu.make_async_remote_copy(
-            src_ref=parts.at[i, chunk(t)], dst_ref=got.at[slot, chunk(t)], send_sem=ps_sem.at[i, t],
+            src_ref=parts.at[i, chunk(t)], dst_ref=got.at[slot, chunk(t)], send_sem=ps_sem.at[i],
             recv_sem=got_sem.at[slot, chunk(t)], device_id=(who, h), device_id_type=MESH,
         )
 
@@ -352,14 +370,14 @@
                 part_own(t).start()
 
     own_first = (lax.rem(c, 4) == 2) & (c >= own_k)
-    pl.when(own_first)(put_own_part)
-
     put(parts.at[0], back_k)
 
     @pl.when(c >= back_k)
     def _():
         for t in order:
             part_back(t).start()
+
+    pl.when(own_first)(put_own_part)
 
     put(back, 2)
 
@@ -387,16 +405,18 @@
         dqr[:, at_pair(j, 2 * ROPE)] = rope
         return carry
 
-    lax.fori_loop(0, heads // 2, dq_step, 0, unroll=2)
     own_ok = even | (c + 3 < n_ctx)
 
     def scatter(t):
         return pltpu.make_async_remote_copy(
-            src_ref=zparts.at[chunk(t)], dst_ref=zgot.at[h], send_sem=ws_sem.at[t],
+            src_ref=zparts.at[chunk(t)], dst_ref=zgot.at[h], send_sem=ws_sem,
             recv_sem=zgot_sem.at[h], device_id=(c, chunk(t)), device_id_type=MESH,
         )
 
-    for t in order:
+    turns = len(order)
+    for i, t in enumerate(order):
+        first, last = ((pairs * (i + turns - 1)) // (2 * turns - 2) if i else 0), (pairs * (i + turns)) // (2 * turns - 2)
+        lax.fori_loop(first, min(last, pairs), dq_step, 0, unroll=True)
 
         @pl.when(own_ok)
         def _():
@@ -415,41 +435,34 @@
     total = own[h]
     for t in range(1, n_head):
         pltpu.make_async_remote_copy(
-            src_ref=zparts.at[h], dst_ref=zgot.at[near(t)], send_sem=ws_sem.at[t],
+            src_ref=zparts.at[h], dst_ref=zgot.at[near(t)], send_sem=ws_sem,
             recv_sem=zgot_sem.at[near(t)], device_id=(c, near(t)), device_id_type=MESH,
         ).wait_recv()
         total = total + zgot[near(t)].astype(F32)
     dlat_ref[...] = total
 
-    for t in range(1, n_head):
-        scatter(t).wait_send()
-        over_head(t).wait_send()
-
-    @pl.when(c + 2 < n_ctx)
-    def _():
-        for t in range(n_head):
-            send_two_ahead(t).wait_send()
-
-    @pl.when(b_ok)
-    def _():
-        for t in range(n_head):
-            send_odd_ahead(t).wait_send()
-
-    @pl.when(c >= 2)
-    def _():
-        for t in range(n_head):
-            forward(t).wait_send()
-            part_next(t).wait_send()
-
-    @pl.when(c >= back_k)
-    def _():
-        for t in range(n_head):
-            part_back(t).wait_send()
-
-    @pl.when(c >= own_k)
-    def _():
-        for t in range(n_head):
-            part_own(t).wait_send()
+    def sent(sem, count):
+        pltpu.make_async_remote_copy(
+            src_ref=win.at[0, pl.ds(0, count)], dst_ref=win.at[0, pl.ds(0, count)], send_sem=sem,
+            recv_sem=win_sem.at[0, 0], device_id=(partner, h), device_id_type=MESH,
+        ).wait_send()
+
+    sent(ws_sem, n_head - 1)
+    sent(zs_sem, n_head - 1)
+    for ok, sem, count in (
+        (c + 2 < n_ctx, as_sem, n_head),
+        (b_ok, bs_sem, n_head),
+        ((c >= 2) & even, cs_sem, late),
+        ((c >= 2) & jnp.logical_not(even), cs_sem, n_head),
+        (direct_ok, ds_sem, n_head - late),
+        (c >= 2, ps_sem.at[2], n_head),
+        (c >= back_k, ps_sem.at[0], n_head),
+        (c >= own_k, ps_sem.at[1], n_head),
+    ):
+
+        @pl.when(ok)
+        def _():
+            sent(sem, count)
 
 
 def write_out(a, b, c, a_hbm, b_hbm, c_hbm, sem):
@@ -499,13 +512,13 @@
             pltpu.VMEM((group, group), F32),
             pltpu.VMEM((span, wide), BF),
             pltpu.VMEM((span, wide), BF),
-            pltpu.VMEM((span, wide), BF),
-            pltpu.VMEM((span, wide), BF),
+            pltpu.VMEM((group, wide), BF),
+            pltpu.VMEM((group, wide), BF),
             pltpu.VMEM((span, heads * group), BF),
             pltpu.VMEM((2, span, 2 * group), F32),
             pltpu.VMEM((2, 8, 2 * group), F32),
             pltpu.VMEM((2, span, 2 * group), F32),
-            pltpu.VMEM((2, span, 2 * group), BF),
+            pltpu.VMEM((span, heads * group), BF),
             pltpu.VMEM(block, F32),
             pltpu.VMEM(block, F32),
             pltpu.VMEM((3,) + block, BF),
@@ -515,14 +528,15 @@
             dma((5,)),
             dma(()),
             dma(()),
-            dma((n_head,)),
-            dma((n_head,)),
-            dma((n_head,)),
-            dma((n_head,)),
+            dma(()),
+            dma(()),
+            dma(()),
+            dma(()),
+            dma(()),
             dma((STEPS + 1, n_head)),
+            dma((3,)),
             dma((3, n_head)),
-            dma((3, n_head)),
-            dma((n_head,)),
+            dma(()),
             dma((n_head,)),
         ],
         compiler_params=pltpu.CompilerParams(collective_id=0, has_side_effects=True),

time: 33.9 us -> 32.9 us (0.971)
  Pallas kernels: 33.2 us -> 32 us
    pallas_call x1, Pallas kernels: 32 us -> 30.8 us  [on_device(): pl.pallas_call(functools.partial(kernel, n_ctx, n_head), out_shape=(pltpu...]
where the time goes in v3:
time: 32.9 us; the launch traced here: 32.6 us
  Pallas kernels  32 us (97%)
  between operations  0.64 us (2%)
    pallas_call x1, Pallas kernels, on_device(): pl.pallas_call(functools.partial(kernel, n_ctx, n_head), out_shape=(pltpu...  30.8 us
    pallas_call x1, Pallas kernels, on_device(): pl.pallas_call(write_out, out_shape=tuple((jax.ShapeDtypeStruct(r.shape,...  1.18 us

profile of v3, /device:TPU:0, one launch (start us, length us, event | category | flops | bytes accessed | tf_op | source)
XLA Modules:
  0.0 32.6 jit_solution(3225288647502821785)
XLA Ops:
  0.6 30.8 %latent_attention_grads.1 = (f32[128,2048]{1,0:T(8,128)S(1)}, f32[128,1024]{1,0:T(8,128)S(1)}, f32[32,576]{1,0:T(8,128)S(1)}) custom-call(s32[1,3]{1,0:T(1,128)} %keep_hbm.1, bf16[32,576]{1,0:T(8,128)(2,1)} %lat_hbm.1, bf16[128,2048]{1,0:T(8,128)(2,1)} %qn_hbm.1, bf16[128,1024]{1,0:T(8,128)(2,1)} %qr_hbm.1, bf16[128,2048]{1,0:T(8,128)(2,1)} %go_hbm.1, ...), custom_call_target="tpu_custom_call" | custom-call | tf_op jit(solution)/shard_map/latent_attention_grads/pallas_call | solution.py:490
  31.4 1.2 %write_out.1 = (f32[128,2048]{1,0:T(8,128)}, f32[128,1024]{1,0:T(8,128)}, f32[32,576]{1,0:T(8,128)}) custom-call(f32[128,2048]{1,0:T(8,128)S(1)} %get-tuple-element.6.a, f32[128,1024]{1,0:T(8,128)S(1)} %get-tuple-element.7.b, f32[32,576]{1,0:T(8,128)S(1)} %get-tuple-element.8.c), custom_call_target="tpu_custom_call" | custom-call | tf_op jit(solution)/shard_map/write_out/pallas_call | solution.py:546
